TPU v7x, 32 devices: a whole 2x2x4 slice. The times are simulated.
32 devices in a mesh: ctx: 4 (over x, core), exp: 8 (over z, y).
Axes of the slice: x: 2, y: 2, z: 4, core: 2. Of those that a mesh axis runs over, the one named last changes fastest.
Arguments:
- q_nope: bfloat16 [128, 128, 512], P('ctx', 'exp'), may hold values from -72 to 72
- q_rope: bfloat16 [128, 8192], P('ctx', 'exp'), may hold values from -6 to 6
- cache_keys: bfloat16 [576, 512], P(None, 'ctx'), may hold values from -6 to 6
- fresh_keys: bfloat16 [576, 128], P(None, 'ctx'), may hold values from -6 to 6
- block_order: int32 [8], replicated, may hold values from 0 to 7, each once
- w_uv: bfloat16 [128, 512, 128], P('exp'), may hold values from -0.25 to 0.25
- w_out: bfloat16 [16384, 7168], P('exp', 'ctx'), may hold values from -0.046875 to 0.046875
- residual: bfloat16 [128, 7168], P(('ctx', 'exp')), may hold values from -6 to 6
- norm_gain: float32 [7168], replicated, may hold values from 0.5 to 1.5
- router_weight: bfloat16 [7168, 16], replicated, may hold values from -0.0625 to 0.0625
- expert_ids: int32 [128, 8], P(('ctx', 'exp')), may hold values from 0 to 15, all different within a row; in each aligned block of 4 rows (0 to 3, 4 to 7, ...) at most 3 rows name the same one
- w_gate: bfloat16 [16, 7168, 2048], P('exp', None, 'ctx'), may hold values from -0.0625 to 0.0625
- w_up: bfloat16 [16, 7168, 2048], P('exp', None, 'ctx'), may hold values from -0.0625 to 0.0625
- w_down: bfloat16 [16, 2048, 7168], P('exp', 'ctx'), may hold values from -0.125 to 0.125
Outputs:
- layer_out: bfloat16 [128, 7168], P(('ctx', 'exp'))
Inputs may be any that keep to these rules, and one draw needn't show every extreme that they name: A permutation: block j of the new tokens (16 rows) sits at positions 512 + block_order[j] * 16 onward. `expert_ids`: each row names 8 different experts; the 4 rows of one device name no expert more than 3 times, and in some aligned block one expert exactly 3 times.
All inputs are finite; a program needn't handle non-finite values.
Results may differ from a plain program's by a relative error of at most 0.012.
Values may be sent and summed in bfloat16 or wider, within the bound.
A program may use at most 128 MiB of HBM per device.

v0:
```python
import functools
import math

import jax
import jax.numpy as jnp
from jax import lax
from jax.experimental import pallas as pl
from jax.experimental.pallas import tpu as pltpu
from jax.sharding import PartitionSpec as P

QKD = 192
VMEM_BYTES = 56 * 1024 * 1024
SPARE_BYTES = 2 * 1024 * 1024

ROUTE_SCALE = 2.5
NORM_EPS = 1e-06


def block_position(row_index, block_order, block_rows):
    blocks = row_index // block_rows
    lookup = blocks[:, None] == jnp.arange(block_order.shape[0], dtype=jnp.int32)[None, :]
    leading = jnp.sum(jnp.where(lookup, block_order[None, :], 0), axis=1)
    return leading * block_rows + row_index % block_rows


def attend(query_lat, query_pe, keys, visible):
    row_count, head_count, latent_width = query_lat.shape
    key_count = keys.shape[1]
    pe_width = query_pe.shape[1] // head_count
    first_dot = jnp.dot(
        query_lat.reshape(row_count * head_count, latent_width),
        keys[:latent_width],
        preferred_element_type=jnp.float32,
    )
    second_dot = jnp.dot(
        query_pe.reshape(row_count * head_count, pe_width),
        keys[latent_width:],
        preferred_element_type=jnp.float32,
    )
    scores = ((first_dot + second_dot) * (1.0 / math.sqrt(QKD))).reshape(
        row_count, head_count, key_count
    )
    scores = jnp.where(visible[:, None, :], scores, -jnp.inf)
    row_max = jnp.max(scores, axis=2)
    exponent = jnp.exp(scores - row_max[:, :, None])
    row_sum = jnp.sum(exponent, axis=2)
    weights = exponent.astype(jnp.bfloat16).reshape(row_count * head_count, key_count)
    latent = lax.dot_general(
        weights, keys[:latent_width], (((1,), (1,)), ((), ())), preferred_element_type=jnp.float32
    )
    return (row_max, row_sum, latent.reshape(row_count, head_count, latent_width))


def remote(src, dst, send, recv, target):
    return pltpu.make_async_remote_copy(
        src_ref=src,
        dst_ref=dst,
        send_sem=send,
        recv_sem=recv,
        device_id=target,
        device_id_type=pl.DeviceIdType.MESH,
    )


def place():
    ctx_count, exp_count = lax.axis_size("ctx"), lax.axis_size("exp")
    ctx, exp = lax.axis_index("ctx"), lax.axis_index("exp")
    return ctx_count // 2, exp_count, ctx, exp, ctx // 2, ctx % 2


def greet(over_exp):
    ctx_count, exp_count = lax.axis_size("ctx"), lax.axis_size("exp")
    ctx, exp = lax.axis_index("ctx"), lax.axis_index("exp")
    barrier = pltpu.get_barrier_semaphore()
    peers = [((ctx + k) % ctx_count, exp) for k in range(1, ctx_count)]
    if over_exp:
        peers += [(ctx, (exp + k) % exp_count) for k in range(1, exp_count)]
    for peer in peers:
        pl.semaphore_signal(
            barrier, inc=1, device_id=peer, device_id_type=pl.DeviceIdType.MESH
        )
    pl.semaphore_wait(barrier, len(peers))


def column_block(rows, wide, ctx, exp, width):
    if not wide:
        return rows.at[ctx, exp]
    return rows.at[exp, :, pl.ds(pl.multiple_of(ctx * width, 128), width)]


def start_gather(src, out, send, recv):
    chips, _, ctx, exp, chip, core = place()
    flights = []
    for k in range(chips):
        peer = ctx + 1 - 2 * core if k == 0 else (chip + k) % chips * 2 + core
        copy = remote(src, out.at[ctx], send.at[0, k], recv.at[0, k], (peer, exp))
        copy.start()
        flights.append(copy)
    return flights


def finish_gather(out, flights, send, recv):
    chips, _, ctx, exp, chip, core = place()
    relayed = []
    for k in range(1, chips):
        flights[k].wait_recv()
        origin = (chip + chips - k) % chips * 2 + core
        copy = remote(
            out.at[origin], out.at[origin], send.at[1, k], recv.at[1, k], (ctx + 1 - 2 * core, exp)
        )
        copy.start()
        relayed.append(copy)
    flights[0].wait_recv()
    for copy in relayed:
        copy.wait_recv()
    for copy in flights + relayed:
        copy.wait_send()


def inputs_kernel(
    cache, fresh, res, ids, cache_out, fresh_out, res_out, ids_out,
    c_send, c_recv, f_send, f_recv, r_send, r_recv, i_send, i_recv, j_send, j_recv,
):
    chips, exp_count, ctx, exp, chip, core = place()
    ctx_count = 2 * chips
    greet(True)
    id_flights = []
    for k in range(1, exp_count):
        copy = remote(
            ids, ids_out.at[ctx, exp], i_send.at[k], i_recv.at[k], (ctx, (exp + k) % exp_count)
        )
        copy.start()
        id_flights.append(copy)
    cache_flights = start_gather(cache, cache_out, c_send, c_recv)
    fresh_flights = start_gather(fresh, fresh_out, f_send, f_recv)
    res_flights = []
    for k in range(1, ctx_count):
        peer = (ctx + k) % ctx_count
        copy = remote(res.at[peer], res_out.at[ctx], r_send.at[k], r_recv.at[k], (peer, exp))
        copy.start()
        res_flights.append(copy)
    cache_out[ctx] = cache[...]
    fresh_out[ctx] = fresh[...]
    res_out[ctx] = res[ctx]
    ids_out[ctx, exp] = ids[...]
    for copy in id_flights:
        copy.wait()
    for k in range(1, ctx_count):
        copy = remote(
            ids_out.at[ctx],
            ids_out.at[ctx],
            j_send.at[k],
            j_recv.at[k],
            ((ctx + k) % ctx_count, exp),
        )
        copy.start()
        res_flights.append(copy)
    finish_gather(cache_out, cache_flights, c_send, c_recv)
    finish_gather(fresh_out, fresh_flights, f_send, f_recv)
    for copy in res_flights:
        copy.wait()


def heads_kernel(src, out, send, recv):
    _, _, ctx, _, _, _ = place()
    greet(False)
    flights = start_gather(src, out, send, recv)
    out[ctx] = src[...]
    finish_gather(out, flights, send, recv)


def hidden_kernel(
    wide, part, res, out, landed, a_send, a_recv, b_send, b_recv, x_send, x_recv, f_send, f_recv
):
    chips, exp_count, ctx, exp, chip, core = place()
    partner = ctx + 1 - 2 * core
    width = part.shape[2]
    place_of = lambda c, e: column_block(out, wide, c, e, width)
    greet(True)
    first = []
    for k in range(1, exp_count):
        peer = (exp + k) % exp_count
        copy = remote(part.at[peer], landed.at[k], a_send.at[k], a_recv.at[k], (ctx, peer))
        copy.start()
        first.append(copy)
    total = part[exp].astype(jnp.float32)
    for k in range(1, exp_count):
        first[k - 1].wait_recv()
        total = total + landed[k].astype(jnp.float32)
    own = place_of(ctx, exp)
    own[...] = (res[...].astype(jnp.float32) + total).astype(jnp.bfloat16)
    pending = []
    spread = [None]
    for k in range(1, exp_count):
        copy = remote(
            own,
            own,
            b_send.at[k],
            b_recv.at[k],
            (ctx, (exp + k) % exp_count),
        )
        copy.start()
        spread.append(copy)
    for k in range(exp_count):
        if k > 0:
            spread[k].wait_recv()
        source = (exp + exp_count - k) % exp_count
        block = place_of(ctx, source)
        row = []
        for p in range(chips):
            peer = partner if p == 0 else (chip + p) % chips * 2 + core
            copy = remote(block, block, x_send.at[p, k], x_recv.at[p, k], (peer, exp))
            copy.start()
            row.append(copy)
        pending.append(row)
    last = []
    for k in range(exp_count):
        source = (exp + exp_count - k) % exp_count
        for p in range(1, chips):
            pending[k][p].wait_recv()
            origin = (chip + chips - p) % chips * 2 + core
            block = place_of(origin, source)
            copy = remote(block, block, f_send.at[p, k], f_recv.at[p, k], (partner, exp))
            copy.start()
            last.append(copy)
    for row in pending:
        row[0].wait_recv()
    for copy in last:
        copy.wait()
    for copy in first + spread[1:] + [copy for row in pending for copy in row]:
        copy.wait_send()


def combine_kernel(
    wide, y, hid, out, pair, cross_out, cross_in, home_out, home_in, final,
    p_send, p_recv, x_send, x_recv, e_send, e_recv, o_send, o_recv,
):
    chips, exp_count, ctx, exp, chip, core = place()
    partner = ctx + 1 - 2 * core
    ctx_count, tok, width = out.shape
    part_of = lambda c, e: column_block(y, wide, c, e, width)
    greet(True)
    order = list(range(1, exp_count)) + [0]
    halves, crossing, homing = {}, {}, {}
    for k in order:
        dest = (exp + k) % exp_count
        for j in list(range(1, chips)) + [0]:
            theirs = (chip + j) % chips * 2 + 1 - core
            copy = remote(
                part_of(theirs, dest),
                pair.at[k, j],
                p_send.at[k, j],
                p_recv.at[k, j],
                (partner, exp),
            )
            copy.start()
            halves[k, j] = copy
    for k in order:
        dest = (exp + k) % exp_count
        for j in range(1, chips):
            owner = (chip + j) % chips * 2 + core
            halves[k, j].wait_recv()
            both = part_of(owner, dest)[...].astype(jnp.float32) + pair[k, j].astype(jnp.float32)
            cross_out[k, j] = both.astype(jnp.bfloat16)
            copy = remote(
                cross_out.at[k, j],
                cross_in.at[k, j],
                x_send.at[k, j],
                x_recv.at[k, j],
                (owner, exp),
            )
            copy.start()
            crossing[k, j] = copy
    total = hid[...].astype(jnp.float32)
    for k in order:
        dest = (exp + k) % exp_count
        halves[k, 0].wait_recv()
        both = part_of(ctx, dest)[...].astype(jnp.float32) + pair[k, 0].astype(jnp.float32)
        for j in range(1, chips):
            crossing[k, j].wait_recv()
            both = both + cross_in[k, j].astype(jnp.float32)
        if k == 0:
            total = total + both
        else:
            home_out[k] = both.astype(jnp.bfloat16)
            copy = remote(
                home_out.at[k], home_in.at[k], e_send.at[k], e_recv.at[k], (ctx, dest)
            )
            copy.start()
            homing[k] = copy
    for k in range(1, exp_count):
        homing[k].wait_recv()
        total = total + home_in[k].astype(jnp.float32)
    for c in range(ctx_count):
        final[c] = total[c * tok : (c + 1) * tok].astype(jnp.bfloat16)
    last = []
    for k in range(1, ctx_count):
        peer = (ctx + k) % ctx_count
        copy = remote(final.at[peer], out.at[ctx], o_send.at[k], o_recv.at[k], (peer, exp))
        copy.start()
        last.append(copy)
    out[ctx] = final[ctx]
    for copy in last:
        copy.wait()
    for copy in list(halves.values()) + list(crossing.values()) + list(homing.values()):
        copy.wait_send()


def exchange(number, kernel, shapes, scratch, *operands):
    vmem = pl.BlockSpec(memory_space=pltpu.VMEM)
    held = jax.tree.leaves(shapes) + list(operands)
    held += [s for s in scratch if s.dtype == jnp.bfloat16]
    need = sum(2 * math.prod(h.shape) * h.dtype.itemsize for h in held) + SPARE_BYTES
    return pl.pallas_call(
        kernel,
        out_shape=shapes,
        in_specs=[vmem] * len(operands),
        out_specs=jax.tree.map(lambda _: vmem, shapes),
        scratch_shapes=scratch,
        compiler_params=pltpu.CompilerParams(
            collective_id=number, has_side_effects=True, vmem_limit_bytes=min(need, VMEM_BYTES)
        ),
    )(*operands)


def body(
    q_nope,
    q_rope,
    cache_keys,
    fresh_keys,
    block_order,
    w_uv,
    w_out,
    residual,
    norm_gain,
    router_weight,
    expert_ids,
    w_gate,
    w_up,
    w_down,
):
    ctx_count = lax.axis_size("ctx")
    exp_count = lax.axis_size("exp")
    ctx_index = lax.axis_index("ctx")
    exp_index = lax.axis_index("exp")
    rows_here, heads_here, latent_width = q_nope.shape
    value_width = w_uv.shape[2]
    key_width, cache_len = cache_keys.shape
    tok_here, model_width = residual.shape
    col_part = w_out.shape[1]
    chips = ctx_count // 2
    block_rows = rows_here * ctx_count // block_order.shape[0]
    dma = pltpu.SemaphoreType.DMA
    bf16 = functools.partial(jax.ShapeDtypeStruct, dtype=jnp.bfloat16)

    res_cols = residual.reshape(tok_here, ctx_count, col_part).transpose(1, 0, 2)
    cache_all, fresh_all, res_own, ids_all = exchange(
        0,
        inputs_kernel,
        (
            bf16((ctx_count, key_width, cache_len)),
            bf16((ctx_count, rows_here, key_width)),
            bf16((ctx_count, tok_here, col_part)),
            jax.ShapeDtypeStruct((ctx_count, exp_count) + expert_ids.shape, jnp.int32),
        ),
        [dma((2, chips))] * 4 + [dma((ctx_count,))] * 2 + [dma((exp_count,))] * 2
        + [dma((ctx_count,))] * 2,
        cache_keys, fresh_keys.T, res_cols, expert_ids,
    )
    cached = jnp.transpose(cache_all, (1, 0, 2)).reshape(key_width, ctx_count * cache_len)
    fresh = fresh_all.reshape(ctx_count * rows_here, key_width).T
    keys = jnp.concatenate([cached, fresh], axis=1)
    own_rows = ctx_index * rows_here + jnp.arange(rows_here, dtype=jnp.int32)
    own_pos = block_position(own_rows, block_order, block_rows)
    new_rows = jnp.arange(ctx_count * rows_here, dtype=jnp.int32)
    key_pos = jnp.concatenate(
        [
            jnp.full((ctx_count * cache_len,), -1, jnp.int32),
            block_position(new_rows, block_order, block_rows),
        ]
    )
    visible = key_pos[None, :] <= own_pos[:, None]
    row_max, row_sum, latent = attend(q_nope, q_rope, keys, visible)
    normal_lat = (latent / row_sum[:, :, None]).astype(jnp.bfloat16)
    head_out = jnp.einsum(
        "rhl,hlv->rhv", normal_lat, w_uv, preferred_element_type=jnp.float32
    ).astype(jnp.bfloat16).reshape(rows_here, heads_here * value_width)
    heads_all = exchange(
        1,
        heads_kernel,
        bf16((ctx_count,) + head_out.shape),
        [dma((2, chips))] * 2,
        head_out,
    )
    heads_all = (
        heads_all.reshape(ctx_count, exp_count, tok_here, -1)
        .transpose(1, 0, 2, 3)
        .reshape(exp_count * ctx_count * tok_here, -1)
    )
    head_partial = jnp.dot(heads_all, w_out, preferred_element_type=jnp.float32)
    group = ctx_count * tok_here
    wide = col_part % 128 == 0
    tokens = exp_count * group
    stripes = (exp_count, group, model_width)
    blocks = (ctx_count, exp_count, group, col_part)
    hidden_all = exchange(
        2,
        functools.partial(hidden_kernel, wide),
        bf16(stripes if wide else blocks),
        [pltpu.VMEM((exp_count, group, col_part), jnp.bfloat16)]
        + [dma((exp_count,))] * 4
        + [dma((chips, exp_count))] * 4,
        head_partial.astype(jnp.bfloat16).reshape(exp_count, group, col_part),
        res_own.reshape(group, col_part),
    )
    if not wide:
        hidden_all = hidden_all.transpose(1, 2, 0, 3)
    hidden_rows = hidden_all.reshape(tokens, model_width)
    hidden = hidden_rows.astype(jnp.float32)
    mean_square = jnp.mean(hidden * hidden, axis=1, keepdims=True)
    normed = (hidden * lax.rsqrt(mean_square + NORM_EPS) * norm_gain).astype(jnp.bfloat16)
    affinity = jax.nn.sigmoid(jnp.dot(normed, router_weight, preferred_element_type=jnp.float32))
    expert_count = router_weight.shape[1]
    ids = ids_all.transpose(1, 0, 2, 3).reshape(tokens, -1)
    onehot = ids[:, :, None] == jnp.arange(expert_count, dtype=jnp.int32)[None, None, :]
    named = jnp.any(onehot, axis=1)
    chosen = jnp.where(named, affinity, 0.0)
    mixing = ROUTE_SCALE * chosen / jnp.sum(chosen, axis=1, keepdims=True)
    local_experts, _, hidden_units = w_gate.shape
    mine = lax.dynamic_slice_in_dim(mixing, exp_index * local_experts, local_experts, axis=1)
    acts = []
    for i in range(local_experts):
        gate = jnp.dot(normed, w_gate[i], preferred_element_type=jnp.float32)
        upward = jnp.dot(normed, w_up[i], preferred_element_type=jnp.float32)
        acts.append((jax.nn.silu(gate) * upward * mine[:, i : i + 1]).astype(jnp.bfloat16))
    acts = jnp.concatenate(acts, axis=1)
    down = w_down.reshape(local_experts * hidden_units, model_width)
    mixed = jnp.dot(acts, down, preferred_element_type=jnp.float32).astype(jnp.bfloat16)
    own_hidden = lax.dynamic_slice(
        hidden_rows, (exp_index * group, ctx_index * col_part), (group, col_part)
    )
    mixed = mixed.reshape(stripes)
    if not wide:
        mixed = mixed.reshape(exp_count, group, ctx_count, col_part).transpose(2, 0, 1, 3)
    block = (group, col_part)
    owned = exchange(
        3,
        functools.partial(combine_kernel, wide),
        bf16((ctx_count, tok_here, col_part)),
        [pltpu.VMEM((exp_count, chips) + block, jnp.bfloat16)] * 3
        + [pltpu.VMEM((exp_count,) + block, jnp.bfloat16)] * 2
        + [pltpu.VMEM((ctx_count, tok_here, col_part), jnp.bfloat16)]
        + [dma((exp_count, chips))] * 4
        + [dma((exp_count,))] * 2
        + [dma((ctx_count,))] * 2,
        mixed,
        own_hidden,
    )
    return owned.transpose(1, 0, 2).reshape(tok_here, model_width)


def solution(mesh):
    return jax.shard_map(
        body,
        mesh=mesh,
        in_specs=(
            P("ctx", "exp", None),
            P("ctx", "exp"),
            P(None, "ctx"),
            P(None, "ctx"),
            P(),
            P("exp", None, None),
            P("exp", "ctx"),
            P(("ctx", "exp"), None),
            P(),
            P(),
            P(("ctx", "exp"), None),
            P("exp", None, "ctx"),
            P("exp", None, "ctx"),
            P("exp", "ctx", None),
        ),
        out_specs=P(("ctx", "exp"), None),
        check_vma=False,
    )
```

profile of v0, /device:TPU:0, one launch (start us, length us, event | category | flops | bytes accessed | tf_op | source)
XLA Modules:
  0.0 117.3 jit_solution(9574012158730810391)
XLA Ops:
  0.0 0.0 copy-start
  0.0 0.9 select_reduce_fusion
  0.9 0.7 select_reduce_fusion.1
  1.7 0.1 broadcast_compare_fusion
  1.8 1.7 %reshape.197 = bf16[512,64]{1,0:T(8,128)(2,1)} reshape(bf16[32,1024]{1,0:T(8,128)(2,1)} %param.15) | data formatting | bytes 131072 | tf_op jit(solution)/shard_map/reshape | solution.py:36
  3.4 0.1 broadcast_in_dim.62
  3.5 0.0 copy-start.2
  3.5 0.9 copy-done.2
  4.4 0.0 copy-start.3
  4.4 0.8 copy-done.3
  5.2 0.0 copy-start.4
  5.2 0.8 copy-done.4
  6.0 0.0 copy-start.5
  6.0 0.7 copy-done.5
  6.7 14.7 %shard_map.136 = (bf16[4,576,128]{2,1,0:T(8,128)(2,1)S(1)}, bf16[4,32,576]{2,1,0:T(8,128)(2,1)S(1)}, bf16[4,4,1792]{2,1,0:T(4,128)(2,1)S(1)}, s32[4,8,4,8]{3,2,1,0:T(4,128)S(1)}) custom-call(bf16[576,128]{1,0:T(8,128)(2,1)S(1)} %copy-done.2, bf16[32,576]{1,0:T(8,128)(2,1)S(1)} %bitcast.90, bf16[4,4,1792]{2,1,0:T(4,128)(2,1)S(1)} %bitcast.89, ...), custom_call_target="tpu_custom_call" | custom-call | tf_op jit(solution)/shard_map/pallas_call | solution.py:314
  21.4 0.1 copy_bitcast_fusion
  21.5 0.1 copy.24
  21.7 0.0 copy-start.6
  21.8 0.6 fusion.60
  22.4 1.6 %fusion.68 = f32[640,512]{0,1:T(8,128)S(1)} fusion(bf16[512,512]{1,0:T(8,128)(2,1)} %bitcast.105, bf16[576,512]{1,0:T(8,128)(2,1)S(1)} %copy_bitcast_fusion, bf16[576,128]{1,0:T(8,128)(2,1)S(1)} %bitcast.101), kind=kOutput, calls=%fused_computation.87 | convolution fusion | flops 336855040 | bytes 2572288 | tf_op jit(solution)/shard_map/dot_general | solution.py:30
  24.0 0.0 copy-done.6
  24.0 0.5 fusion.70
  24.5 0.4 fusion.35
  24.9 0.7 div.60
  25.6 0.8 copy.26
  26.3 0.0 copy-done
  26.3 1.5 %fusion.44 = bf16[16,4,8,128]{3,2,1,0:T(8,128)(2,1)} fusion(bf16[16,512,128]{2,1,0:T(8,128)(2,1)S(1)} %copy-done, bf16[32,16,640]{2,1,0:T(8,128)(2,1)S(1)} %bitcast.100, f32[32,16]{0,1:T(8,128)S(1)} %copy.26, bf16[576,512]{1,0:T(8,128)(2,1)S(1)} %copy_bitcast_fusion, bf16[576,128]{1,0:T(8,128)(2,1)S(1)} %bitcast.103), kind=kOutput, calls=%fused_computation.40 | convolution fusion | flops 404553728 | bytes 3622912 | tf_op jit(solution)/shard_map/rhl,hlv->rhv/dot_general | solution.py:385
  27.9 0.9 copy.40
  28.8 6.9 %shard_map.137 = bf16[4,32,2048]{2,1,0:T(8,128)(2,1)S(1)} custom-call(bf16[32,2048]{1,0:T(8,128)(2,1)S(1)} %bitcast.85), custom_call_target="tpu_custom_call" | custom-call | tf_op jit(solution)/shard_map/pallas_call | solution.py:314
  35.7 0.2 reshape.199
  35.9 0.2 copy.39
  36.2 0.1 reshape.200
  36.3 4.2 %convolution_convert_fusion.1 = bf16[128,1792]{1,0:T(8,128)(2,1)S(1)} fusion(bf16[128,2048]{1,0:T(8,128)(2,1)S(1)} %reshape.200, bf16[2048,1792]{1,0:T(8,128)(2,1)} %param.20), kind=kOutput, calls=%fused_computation.19 | convolution fusion | flops 939753472 | bytes 8323072 | tf_op jit(solution)/shard_map/dot_general | solution.py:400
  40.5 0.0 copy-start.7
  40.5 0.0 copy-start.8
  40.5 0.0 copy-start.9
  40.5 29.3 %shard_map.138 = bf16[8,16,7168]{2,1,0:T(8,128)(2,1)S(1)} custom-call(bf16[8,16,1792]{2,1,0:T(8,128)(2,1)S(1)} %bitcast.84, bf16[16,1792]{1,0:T(8,128)(2,1)S(1)} %reshape.202.res), custom_call_target="tpu_custom_call" | custom-call | tf_op jit(solution)/shard_map/pallas_call | solution.py:314
  69.9 0.4 fusion.12
  70.3 0.1 rsqrt.13
  70.4 0.0 copy-done.7
  70.4 0.0 copy-done.8
  70.4 0.0 copy-done.9
  70.5 0.7 fusion.71
  71.2 0.5 fusion.14
  71.7 4.2 %fusion.2 = f32[128,512]{1,0:T(8,128)S(1)} fusion(bf16[128,7168]{1,0:T(8,128)(2,1)S(1)} %bitcast.95, bf16[2,7168,512]{2,1,0:T(8,128)(2,1)} %param.25), kind=kOutput, calls=%fused_computation.3 | convolution fusion | flops 939524096 | bytes 9437184 | tf_op jit(solution)/shard_map/dot_general | solution.py:433
  75.9 0.0 slice-start
  76.0 0.0 slice-start.1
  76.0 4.4 %fusion.38 = bf16[128,512]{1,0:T(8,128)(2,1)S(1)} fusion(bf16[128,7168]{1,0:T(8,128)(2,1)S(1)} %bitcast.96, bf16[2,7168,512]{2,1,0:T(8,128)(2,1)} %param.26, f32[128,512]{1,0:T(8,128)S(1)} %fusion.2, f32[128]{0:T(128)S(1)} %get-tuple-element.16), kind=kOutput, calls=%fused_computation.38 | convolution fusion | flops 939982848 | bytes 9568768 | tf_op jit(solution)/shard_map/dot_general | solution.py:434
  80.3 0.0 slice-start.2
  80.3 4.4 %fusion.6 = f32[128,512]{1,0:T(8,128)S(1)} fusion(bf16[128,7168]{1,0:T(8,128)(2,1)S(1)} %bitcast.97, bf16[2,7168,512]{2,1,0:T(8,128)(2,1)} %param.25), kind=kOutput, calls=%fused_computation.7 | convolution fusion | flops 939524096 | bytes 9437184 | tf_op jit(solution)/shard_map/dot_general | solution.py:433
  84.7 0.0 slice-start.3
  84.7 4.4 %fusion.41 = bf16[128,512]{1,0:T(8,128)(2,1)S(1)} fusion(bf16[128,7168]{1,0:T(8,128)(2,1)S(1)} %bitcast.98, bf16[2,7168,512]{2,1,0:T(8,128)(2,1)} %param.26, f32[128,512]{1,0:T(8,128)S(1)} %fusion.6, f32[128]{0:T(128)S(1)} %get-tuple-element.15), kind=kOutput, calls=%fused_computation.39 | convolution fusion | flops 939982848 | bytes 9568768 | tf_op jit(solution)/shard_map/dot_general | solution.py:434
  89.1 0.0 slice-done
  89.1 0.0 slice-done.1
  89.1 0.0 slice-done.2
  89.1 0.0 slice-done.3
  89.1 0.0 copy-start.1
  89.2 2.1 %convolution_convert_fusion = bf16[128,7168]{1,0:T(8,128)(2,1)S(1)} fusion(bf16[1024,7168]{1,0:T(8,128)(2,1)S(1)} %bitcast.93, bf16[128,512]{1,0:T(8,128)(2,1)S(1)} %fusion.38, bf16[128,512]{1,0:T(8,128)(2,1)S(1)} %fusion.41), kind=kOutput, calls=%fused_computation | convolution fusion | flops 1880489984 | bytes 16777216 | tf_op jit(solution)/shard_map/dot_general | solution.py:438
  91.2 25.4 %shard_map.139 = bf16[4,4,1792]{2,1,0:T(4,128)(2,1)S(1)} custom-call(bf16[8,16,7168]{2,1,0:T(8,128)(2,1)S(1)} %bitcast.83, bf16[16,1792]{1,0:T(8,128)(2,1)S(1)} %dynamic_slice.7.hid), custom_call_target="tpu_custom_call" | custom-call | tf_op jit(solution)/shard_map/pallas_call | solution.py:314
  116.6 0.6 copy.42
  117.3 0.0 copy-done.1
  (13 shorter events, 0.2 us)
Async XLA Ops:
  0.0 26.3 %copy-start = (bf16[16,512,128]{2,1,0:T(8,128)(2,1)S(1)}, bf16[16,512,128]{2,1,0:T(8,128)(2,1)}, u32[]{:S(2)}) copy-start(bf16[16,512,128]{2,1,0:T(8,128)(2,1)} %param.19) | copy-start | bytes 6291460
  3.5 0.9 copy-start.2
  4.4 0.8 copy-start.3
  5.2 0.8 copy-start.4
  6.0 0.7 copy-start.5
  21.7 2.3 %copy-start.6 = (bf16[512,64]{1,0:T(8,128)(2,1)S(1)}, bf16[512,64]{1,0:T(8,128)(2,1)}, u32[]{:S(2)}) copy-start(bf16[512,64]{1,0:T(8,128)(2,1)} %reshape.197) | copy-start | bytes 196612
  40.5 29.9 %copy-start.7 = (f32[7168]{0:T(1024)S(1)}, f32[7168]{0:T(1024)}, u32[]{:S(2)}) copy-start(f32[7168]{0:T(1024)} %param.22) | copy-start | bytes 86020
  40.5 29.9 %copy-start.8 = (pred[128,16]{0,1:T(8,128)(4,1)S(1)}, pred[128,16]{0,1:T(8,128)(4,1)}, u32[]{:S(2)}) copy-start(pred[128,16]{0,1:T(8,128)(4,1)} %fusion.60) | copy-start | bytes 6148
  40.5 29.9 %copy-start.9 = (bf16[7168,16]{0,1:T(8,128)(2,1)S(1)}, bf16[7168,16]{0,1:T(8,128)(2,1)}, u32[]{:S(2)}) copy-start(bf16[7168,16]{0,1:T(8,128)(2,1)} %param.23) | copy-start | bytes 688132
  75.9 13.2 %slice-start = ((s8[14680064]{0:T(1024)(128)(4,1)}), s8[4194304]{0:T(1024)(128)(4,1)S(1)}, s32[]{:S(2)}) async-start(s8[14680064]{0:T(1024)(128)(4,1)} %bitcast.91), calls=%async_computation | async-start | bytes 8388608
  76.0 13.2 %slice-start.1 = ((s8[14680064]{0:T(1024)(128)(4,1)}), s8[4194304]{0:T(1024)(128)(4,1)S(1)}, s32[]{:S(2)}) async-start(s8[14680064]{0:T(1024)(128)(4,1)} %bitcast.91), calls=%async_computation.1 | async-start | bytes 8388608
  80.3 8.8 %slice-start.2 = ((s8[14680064]{0:T(1024)(128)(4,1)}), s8[4194304]{0:T(1024)(128)(4,1)S(1)}, s32[]{:S(2)}) async-start(s8[14680064]{0:T(1024)(128)(4,1)} %bitcast.91), calls=%async_computation.2 | async-start | bytes 8388608
  84.7 4.4 %slice-start.3 = ((s8[14680064]{0:T(1024)(128)(4,1)}), s8[2097152]{0:T(1024)(128)(4,1)S(1)}, s32[]{:S(2)}) async-start(s8[14680064]{0:T(1024)(128)(4,1)} %bitcast.91), calls=%async_computation.3 | async-start | bytes 4194304
  89.1 28.1 %copy-start.1 = (bf16[16,512,128]{2,1,0:T(8,128)(2,1)S(1)}, bf16[16,512,128]{2,1,0:T(8,128)(2,1)}, u32[]{:S(2)}) copy-start(bf16[16,512,128]{2,1,0:T(8,128)(2,1)} %param.19) | copy-start | bytes 6291460
where the time goes:
time: 118 us; the launch traced here: 117 us
  Pallas kernels  76.3 us (65%)
  matrix products  27.9 us (24%)
  local copies, waits for them, and re-layouts  8.98 us (8%)
  other arithmetic  3.7 us (3%)
    pallas_call x4, Pallas kernels, exchange(): pl.pallas_call(kernel, out_shape=shapes, in_specs=[vmem] * len(operands),...  76.3 us
    dot_general x2, matrix products, body(): upward = jnp.dot(normed, w_up[i], preferred_element_type=jnp.float32)  8.73 us
    dot_general x2, matrix products, body(): gate = jnp.dot(normed, w_gate[i], preferred_element_type=jnp.float32)  8.56 us
    dot_general x1, matrix products, body(): head_partial = jnp.dot(heads_all, w_out, preferred_element_type=jnp.float32)  4.21 us
    unnamed x29, local copies, waits for them, and re-layouts  3.87 us

commit v1 on v0

--- a/solution.py
+++ b/solution.py
@@ -1,5 +1,6 @@
 import functools
 import math
+import types
 
 import jax
 import jax.numpy as jnp
@@ -323,7 +324,7 @@
     )(*operands)
 
 
-def body(
+def staged_body(
     q_nope,
     q_rope,
     cache_keys,
@@ -459,6 +460,575 @@
     return owned.transpose(1, 0, 2).reshape(tok_here, model_width)
 
 
+GROUPS = 4
+FOLD = 2
+
+
+def widths(total, unit, parts):
+    tiles = total // unit
+    return [(tiles // parts + (1 if i < tiles % parts else 0)) * unit for i in range(parts)]
+
+
+def offsets(sizes):
+    return [sum(sizes[:i]) for i in range(len(sizes))]
+
+
+def fits(ctx_count, exp_count, q_nope, cache_keys, w_uv, w_out, residual, w_gate, block_rows):
+    rows, heads, lat = q_nope.shape
+    weights = 2 * (math.prod(w_uv.shape) + math.prod(w_out.shape) + 3 * math.prod(w_gate.shape))
+    return (
+        ctx_count == 4
+        and exp_count % FOLD == 0
+        and residual.shape[0] * exp_count == rows
+        and residual.shape[0] * ctx_count % 8 == 0
+        and heads % GROUPS == 0
+        and rows % 16 == 0
+        and rows % block_rows == 0
+        and w_out.shape[1] % 256 == 0
+        and cache_keys.shape[1] % 128 == 0
+        and lat % 128 == 0
+        and w_gate.shape[2] % 128 == 0
+        and weights < 54 * 1024 * 1024
+        and residual.shape[1] % 1024 == 0
+        and w_out.shape[1] >= 1024
+        and residual.shape[1] // 1024 * rows * ctx_count <= w_out.shape[0]
+    )
+
+
+def onehot(shape, source):
+    row = lax.broadcasted_iota(jnp.int32, shape, 0)
+    col = lax.broadcasted_iota(jnp.int32, shape, 1)
+    return jnp.where(col == source(row), 1.0, 0.0).astype(jnp.bfloat16)
+
+
+def mm(a, b):
+    return jnp.dot(a, b, preferred_element_type=jnp.float32)
+
+
+def mm_t(a, b):
+    return lax.dot_general(a, b, (((1,), (1,)), ((), ())), preferred_element_type=jnp.float32)
+
+
+def fused_kernel(
+    names, dims,
+    q_nope, q_rope, cache, fresh, order, w_uv, w_out, res, gain, router, ids, w_gate, w_up, w_down,
+    out, *refs,
+):
+    s = types.SimpleNamespace(**dict(zip(names, refs)))
+    d = dims
+    bf16, f32 = jnp.bfloat16, jnp.float32
+    ctx, exp = lax.axis_index("ctx"), lax.axis_index("exp")
+    C, E, Z = d.ctx_count, d.exp_count, d.exp_count // FOLD
+    x, core = ctx // 2, ctx % 2
+    z, y = exp // FOLD, exp % FOLD
+    xctx = (1 - x) * 2 + core
+    partner = (ctx + 1 - 2 * core, exp)
+    xpeer = (xctx, exp)
+    ypeer = (ctx, z * FOLD + 1 - y)
+    zpeer = lambda j: (ctx, (z + j) % Z * FOLD + y)
+    rows, heads, lat, rope = d.rows, d.heads, d.lat, d.rope
+    vals, col, tok, tokens = d.vals, d.col, d.tok, d.tokens
+    group = C * tok
+    hg = heads // GROUPS
+    sent = []
+
+    def push(src, dst, sems, index, target):
+        send, recv = sems
+        copy = remote(src, dst, send.at[index], recv.at[index], target)
+        copy.start()
+        sent.append(copy)
+        return copy
+
+    def load(src, dst, index):
+        copy = pltpu.make_async_copy(src, dst, s.load.at[index])
+        copy.start()
+        return copy
+
+    lanes = lambda start, size: pl.ds(pl.multiple_of(start, 128), size)
+
+    l_cache = load(cache, s.kall.at[:, lanes(ctx * d.cached, d.cached)], 0)
+    l_fresh = load(fresh, s.kfresh.at[pl.ds(pl.multiple_of(ctx * rows, 16), rows)], 1)
+    l_res = load(res, s.res, 2)
+    l_ids = load(ids, s.ids, 3)
+    l_order = load(order, s.order, 4)
+    l_q = load(q_nope, s.qn, 5)
+    l_qr = load(q_rope, s.qr, 6)
+    l_uv = load(w_uv, s.wuv, 7)
+    l_gain = load(gain, s.gain, 8)
+    l_router = load(router, s.router, 9)
+    l_out = load(w_out, s.wout, 10)
+    l_gate = load(w_gate, s.wg, 11)
+    l_up = load(w_up, s.wu, 12)
+    l_down = load(w_down, s.wd, 13)
+    greet(True)
+
+    l_cache.wait()
+    l_fresh.wait()
+    key_sems = (s.k_send, s.k_recv)
+
+    def send_keys(owner, index, target):
+        a = s.kall.at[:, lanes(owner * d.cached, d.cached)]
+        b = s.kfresh.at[pl.ds(pl.multiple_of(owner * rows, 16), rows)]
+        return [push(a, a, key_sems, (0, index), target), push(b, b, key_sems, (1, index), target)]
+
+    k_cross = send_keys(ctx, 0, xpeer)
+    k_pair = send_keys(ctx, 1, partner)
+
+    l_res.wait()
+    r_flights = []
+    for k in range(1, C):
+        peer = (ctx + k) % C
+        r_flights.append(
+            push(s.res.at[:, lanes(peer * col, col)], s.rin.at[ctx], (s.r_send, s.r_recv), k, (peer, exp))
+        )
+    s.rin[ctx] = s.res[:, lanes(ctx * col, col)]
+    l_ids.wait()
+    named = jnp.zeros((tok, 128), f32)
+    lane = lax.broadcasted_iota(jnp.int32, (tok, 128), 1)
+    for k in range(d.top):
+        named = named + jnp.where(s.ids[:, k : k + 1] == lane, 1.0, 0.0)
+    s.nsrc[...] = jnp.zeros((8, 128), f32)
+    s.nsrc[0:tok, :] = named
+    n_flights = [
+        push(s.nsrc, s.nall.at[exp, ctx], (s.n_send, s.n_recv), k, (ctx, (exp + k) % E))
+        for k in range(1, E)
+    ]
+    s.nall[exp, ctx] = s.nsrc[...]
+
+    l_q.wait()
+    for g in range(GROUPS):
+        part = hg * rows
+        perm = onehot((part, rows * heads), lambda i: (i % rows) * heads + g * hg + i // rows)
+        s.qh[g * part : (g + 1) * part, :] = mm(perm, s.qn[...]).astype(bf16)
+    l_qr.wait()
+    for h in range(heads):
+        s.qrh[h * rows : (h + 1) * rows, :] = s.qr[:, h * rope : (h + 1) * rope]
+
+    l_order.wait()
+    size = d.block
+    own_blocks = rows // size
+    part = hg * rows
+    row_id = lax.broadcasted_iota(jnp.int32, (part, tokens), 0) % rows
+    key_id = lax.broadcasted_iota(jnp.int32, (part, tokens), 1)
+    own_pos = row_id % size
+    key_pos = key_id % size
+    for b in range(own_blocks):
+        own_pos = own_pos + jnp.where(row_id // size == b, s.order[ctx * own_blocks + b] * size, 0)
+    for b in range(tokens // size):
+        key_pos = key_pos + jnp.where(key_id // size == b, s.order[b] * size, 0)
+    s.bias[...] = jnp.where(key_pos <= own_pos, 0.0, -jnp.inf)
+
+    for copy in n_flights:
+        copy.wait_recv()
+    n_last = []
+    for k in range(1, C):
+        view = s.nall.at[:, ctx]
+        n_last.append(push(view, view, (s.m_send, s.m_recv), k, ((ctx + k) % C, exp)))
+
+    for copy in k_cross:
+        copy.wait_recv()
+    k_far = send_keys(xctx, 2, partner)
+    for copy in k_pair + k_far:
+        copy.wait_recv()
+
+    scale = 1.0 / math.sqrt(QKD)
+    l_uv.wait()
+    h_cross, h_pair = [], []
+    for g in range(GROUPS):
+        q = s.qh[g * part : (g + 1) * part, :]
+        qr = s.qrh[g * part : (g + 1) * part, :]
+        old = (mm(q, s.kall[0:lat, :]) + mm(qr, s.kall[lat : lat + rope, :])) * scale
+        new = (mm_t(q, s.kfresh[:, 0:lat]) + mm_t(qr, s.kfresh[:, lat : lat + rope])) * scale
+        new = new + s.bias[...]
+        top = jnp.maximum(jnp.max(old, axis=1, keepdims=True), jnp.max(new, axis=1, keepdims=True))
+        old = jnp.exp(old - top)
+        new = jnp.exp(new - top)
+        total = jnp.sum(old, axis=1, keepdims=True) + jnp.sum(new, axis=1, keepdims=True)
+        latent = mm_t(old.astype(bf16), s.kall[0:lat, :]) + mm(new.astype(bf16), s.kfresh[:, 0:lat])
+        latent = (latent / total).astype(bf16)
+        for h in range(hg):
+            one = mm(latent[h * rows : (h + 1) * rows], s.wuv[g * hg + h])
+            s.heads[ctx, g, :, h * vals : (h + 1) * vals] = one.astype(bf16)
+        view = s.heads.at[ctx, g]
+        h_cross.append(push(view, view, (s.h_send, s.h_recv), (0, g), xpeer))
+        h_pair.append(push(view, view, (s.h_send, s.h_recv), (1, g), partner))
+    h_far = []
+    for g in range(GROUPS):
+        h_cross[g].wait_recv()
+        view = s.heads.at[xctx, g]
+        h_far.append(push(view, view, (s.h_send, s.h_recv), (2, g), partner))
+
+    l_out.wait()
+    deep = hg * vals
+    for g in range(GROUPS):
+        h_pair[g].wait_recv()
+        h_far[g].wait_recv()
+        value = mm(s.heads[:, g].reshape(tokens, deep), s.wout[g * deep : (g + 1) * deep, :])
+        if g == 0:
+            s.pacc[...] = value
+        else:
+            s.pacc[...] = s.pacc[...] + value
+
+    chunks = d.chunks
+    starts = offsets(chunks)
+    to_group = onehot(
+        (tokens, tokens), lambda i: (i // tok) % C * rows + i // group * tok + i % tok
+    )
+    y_flights = []
+    for q, (o, w) in enumerate(zip(starts, chunks)):
+        value = mm(to_group, s.pacc[:, o : o + w].astype(bf16)).astype(bf16)
+        s.p[:, :, :, o : o + w] = value.reshape(Z, FOLD, group, w)
+        y_flights.append(
+            push(
+                s.p.at[:, 1 - y, :, pl.ds(o, w)], s.yin.at[:, :, pl.ds(o, w)],
+                (s.y_send, s.y_recv), q, ypeer,
+            )
+        )
+    z_flights = []
+    for q, (o, w) in enumerate(zip(starts, chunks)):
+        y_flights[q].wait_recv()
+        both = s.p[:, y, :, o : o + w].astype(f32) + s.yin[:, :, o : o + w].astype(f32)
+        s.zsrc[:, :, o : o + w] = both.astype(bf16)
+        z_flights.append([
+            push(
+                s.zsrc.at[(z + j) % Z, :, pl.ds(o, w)], s.zin.at[j, :, pl.ds(o, w)],
+                (s.z_send, s.z_recv), (q, j), zpeer(j),
+            )
+            for j in range(1, Z)
+        ])
+    for copy in r_flights:
+        copy.wait_recv()
+    for c in range(C):
+        s.rsum[c * tok : (c + 1) * tok, :] = s.rin[c].astype(f32)
+
+    def block(c, e, q):
+        return s.hid.at[e, :, lanes(c * col + starts[q], chunks[q])]
+
+    gather = {}
+
+    def spread(q, step, index, c, e, target):
+        view = block(c, e, q)
+        gather[q, step, index] = push(view, view, (s.g_send, s.g_recv), (q, d.slot[step, index]), target)
+
+    def axes(q):
+        return (ypeer, xpeer) if q % 2 == 0 else (xpeer, ypeer)
+
+    def near(q, j):
+        return ctx, (z + Z - j) % Z * FOLD + y
+
+    def first(q, j):
+        c, e = near(q, j)
+        return (c, e + 1 - 2 * y) if q % 2 == 0 else (xctx, e)
+
+    def second(q, i):
+        if q % 2 == 0:
+            return xctx, (near(q, i) if i < Z else first(q, i - Z))[1]
+        c, e = near(q, i) if i < Z else first(q, i - Z)
+        return c, e + 1 - 2 * y
+
+    def open_gather(q):
+        c, e = near(q, 0)
+        for j in range(1, Z):
+            spread(q, "z", j, c, e, zpeer(j))
+        a, b = axes(q)
+        spread(q, "a", 0, c, e, a)
+        spread(q, "b", 0, c, e, b)
+        spread(q, "d", 0, c, e, partner)
+
+    def pass_near(q):
+        a, b = axes(q)
+        for j in range(1, Z):
+            gather[q, "z", j].wait_recv()
+            c, e = near(q, j)
+            spread(q, "a", j, c, e, a)
+            spread(q, "b", j, c, e, b)
+            spread(q, "d", j, c, e, partner)
+
+    def pass_first(q):
+        _, b = axes(q)
+        for j in range(Z):
+            gather[q, "a", j].wait_recv()
+            c, e = first(q, j)
+            spread(q, "b", Z + j, c, e, b)
+            spread(q, "d", Z + j, c, e, partner)
+
+    def pass_second(q):
+        for i in range(2 * Z):
+            gather[q, "b", i].wait_recv()
+            c, e = second(q, i)
+            spread(q, "d", 2 * Z + i, c, e, partner)
+
+    def close_gather(q):
+        for i in range(4 * Z):
+            gather[q, "d", i].wait_recv()
+
+    for q, (o, w) in enumerate(zip(starts, chunks)):
+        for copy in z_flights[q]:
+            copy.wait_recv()
+        both = s.p[z, y, :, o : o + w].astype(f32) + s.yin[z, :, o : o + w].astype(f32)
+        for j in range(1, Z):
+            both = both + s.zin[j, :, o : o + w].astype(f32)
+        both = both + s.rsum[:, o : o + w]
+        s.hid[exp, :, lanes(ctx * col + o, w)] = both.astype(bf16)
+        open_gather(q)
+
+    l_gain.wait()
+    l_router.wait()
+    l_gate.wait()
+    l_up.wait()
+    s.ss[...] = jnp.zeros(s.ss.shape, f32)
+    s.racc[...] = jnp.zeros(s.racc.shape, f32)
+    s.gacc[...] = jnp.zeros(s.gacc.shape, f32)
+    s.uacc[...] = jnp.zeros(s.uacc.shape, f32)
+    units = d.units
+
+    def consume(q):
+        w = chunks[q]
+
+        def one(i, carry):
+            c = (ctx + i) % C
+            at = lanes(c * col + starts[q], w)
+            hidden = s.hid[:, :, at].reshape(tokens, w).astype(f32)
+            square = hidden * hidden
+            some = square[:, 0:128]
+            for k in range(1, w // 128):
+                some = some + square[:, k * 128 : (k + 1) * 128]
+            s.ss[...] = s.ss[...] + some
+            scaled = (hidden * s.gain[:, at]).astype(bf16)
+            s.racc[...] = s.racc[...] + mm_t(scaled, s.router[:, at])
+            for k in range(d.local):
+                here = slice(k * units, (k + 1) * units)
+                s.gacc[:, here] = s.gacc[:, here] + mm(scaled, s.wg[k, at, :])
+                s.uacc[:, here] = s.uacc[:, here] + mm(scaled, s.wu[k, at, :])
+            return carry
+
+        lax.fori_loop(0, C, one, 0)
+
+    count = len(chunks)
+    for q in range(count):
+        pass_near(q)
+        pass_first(q)
+    for q in range(count):
+        pass_second(q)
+        close_gather(q)
+        if q > 0:
+            consume(q - 1)
+    consume(count - 1)
+
+    for copy in n_last:
+        copy.wait_recv()
+    squeeze = onehot((tokens, tokens // tok * 8), lambda i: i // tok * 8 + i % tok)
+    named = mm(squeeze, s.nall[...].reshape(tokens // tok * 8, 128).astype(bf16))
+    named = named[:, 0 : d.experts]
+    mean = jnp.sum(s.ss[...], axis=1, keepdims=True) * (1.0 / d.width)
+    factor = lax.rsqrt(mean + NORM_EPS)
+    affinity = jax.nn.sigmoid(s.racc[...] * factor)
+    chosen = jnp.where(named > 0.5, affinity, 0.0)
+    mixing = ROUTE_SCALE * chosen / jnp.sum(chosen, axis=1, keepdims=True)
+    which = lax.broadcasted_iota(jnp.int32, (tokens, d.experts), 1)
+    for k in range(d.local):
+        here = slice(k * units, (k + 1) * units)
+        mine = jnp.sum(jnp.where(which == exp * d.local + k, mixing, 0.0), axis=1, keepdims=True)
+        gate = s.gacc[:, here] * factor
+        upward = s.uacc[:, here] * factor
+        s.acts[:, here] = (gate * jax.nn.sigmoid(gate) * upward * mine).astype(bf16)
+
+    def owner_order(i):
+        t, zz, yy = i % tok, i // tok % Z, i // (tok * Z) % FOLD
+        xx, kk = i // (tok * Z * FOLD) % 2, i // (tok * Z * FOLD * 2)
+        return (zz * FOLD + yy) * group + (xx * 2 + kk) * tok + t
+
+    to_owner = onehot((tokens, tokens), owner_order)
+    for k in range(d.local):
+        here = slice(k * units, (k + 1) * units)
+        s.acts[:, here] = mm(to_owner, s.acts[:, here]).astype(bf16)
+    l_down.wait()
+    cw, n = d.out_width, d.width // d.out_width
+    half, quarter, eighth = tokens // 2, tokens // 4, tokens // 8
+    pairs, hops, lasts, ends = {}, {}, {}, {}
+
+    def produce(i):
+        mixed = mm(s.acts[...], s.wd[:, i * cw : (i + 1) * cw]).astype(bf16)
+        s.wout[i * tokens : (i + 1) * tokens, 0:cw] = mixed
+        away = s.wout.at[pl.ds(pl.multiple_of(i * tokens + (1 - core) * half, 16), half), pl.ds(0, cw)]
+        pairs[i] = push(away, s.pair.at[i], (s.p_send, s.p_recv), i, partner)
+
+    def join_pair(i):
+        pairs[i].wait_recv()
+        mine = s.wout[pl.ds(pl.multiple_of(i * tokens + core * half, 16), half), 0:cw]
+        both = mine.astype(f32) + s.pair[i].astype(f32)
+        s.s1[i] = both.astype(bf16).reshape(2, FOLD, eighth, cw)
+        if i % 2 == 0:
+            hops[i] = push(s.s1.at[i, 1 - x], s.h1.at[i], (s.a_send, s.a_recv), i, xpeer)
+        else:
+            hops[i] = push(s.s1.at[i, :, 1 - y], s.h1.at[i], (s.a_send, s.a_recv), i, ypeer)
+
+    def join_hop(i):
+        hops[i].wait_recv()
+        mine = s.s1[i, x] if i % 2 == 0 else s.s1[i, :, y]
+        s.s2[i] = (mine.astype(f32) + s.h1[i].astype(f32)).astype(bf16)
+        if i % 2 == 0:
+            lasts[i] = push(s.s2.at[i, 1 - y], s.h2.at[i], (s.b_send, s.b_recv), i, ypeer)
+        else:
+            lasts[i] = push(s.s2.at[i, 1 - x], s.h2.at[i], (s.b_send, s.b_recv), i, xpeer)
+
+    def join_last(i):
+        lasts[i].wait_recv()
+        mine = s.s2[i, y] if i % 2 == 0 else s.s2[i, x]
+        s.total[...] = mine.astype(f32) + s.h2[i].astype(f32)
+        for zz in range(Z):
+            s.zo[i, zz] = s.total[zz * tok : (zz + 1) * tok, :].astype(bf16)
+        ends[i] = [
+            push(s.zo.at[i, (z + j) % Z], s.zi.at[i, j], (s.e_send, s.e_recv), (i, j), zpeer(j))
+            for j in range(1, Z)
+        ]
+
+    def finish(i):
+        at = slice(i * cw, (i + 1) * cw)
+        s.total[...] = s.hid[exp, :, at].astype(f32)
+        value = s.zo[i, z].astype(f32)
+        for c in range(C):
+            value = value + jnp.where(ctx == c, s.total[c * tok : (c + 1) * tok, :], 0.0)
+        for j in range(1, Z):
+            ends[i][j - 1].wait_recv()
+            value = value + s.zi[i, j].astype(f32)
+        out[:, at] = value.astype(bf16)
+
+    lag = 3
+    for i in range(n):
+        produce(i)
+        if i >= lag:
+            join_pair(i - lag)
+    for i in range(max(n - lag, 0), n):
+        join_pair(i)
+    for i in range(n):
+        join_hop(i)
+    for i in range(n):
+        join_last(i)
+    for i in range(n):
+        finish(i)
+    for copy in sent:
+        copy.wait_send()
+
+
+def fused_body(dims, arguments):
+    (
+        q_nope, q_rope, cache_keys, fresh_keys, block_order, w_uv, w_out, residual, norm_gain,
+        router_weight, expert_ids, w_gate, w_up, w_down,
+    ) = arguments
+    d = dims
+    bf16, f32 = jnp.bfloat16, jnp.float32
+    dma = pltpu.SemaphoreType.DMA
+    vmem = pltpu.VMEM
+    C, E, Z, Y = d.ctx_count, d.exp_count, d.exp_count // FOLD, FOLD
+    group = C * d.tok
+    keys = d.lat + d.rope
+    n = d.width // d.out_width
+    queries = d.rows * d.heads
+    part = queries // GROUPS
+    hidden = d.local * d.units
+    q = len(d.chunks)
+    scratch = dict(
+        wuv=vmem(w_uv.shape, bf16),
+        wout=vmem(w_out.shape, bf16),
+        wg=vmem(w_gate.shape, bf16),
+        wu=vmem(w_up.shape, bf16),
+        wd=vmem((hidden, d.width), bf16),
+        qn=vmem((queries, d.lat), bf16),
+        qh=vmem((queries, d.lat), bf16),
+        qr=vmem(q_rope.shape, bf16),
+        qrh=vmem((queries, d.rope), bf16),
+        kall=vmem((keys, C * d.cached), bf16),
+        kfresh=vmem((d.tokens, keys), bf16),
+        bias=vmem((part, d.tokens), f32),
+        res=vmem(residual.shape, bf16),
+        rin=vmem((C, d.tok, d.col), bf16),
+        rsum=vmem((group, d.col), f32),
+        ids=vmem(expert_ids.shape, jnp.int32),
+        nsrc=vmem((8, 128), f32),
+        nall=vmem((E, C, 8, 128), f32),
+        order=pltpu.SMEM(block_order.shape, jnp.int32),
+        gain=vmem((1, d.width), f32),
+        router=vmem((d.experts, d.width), bf16),
+        heads=vmem((C, GROUPS, d.rows, d.heads // GROUPS * d.vals), bf16),
+        pacc=vmem((d.tokens, d.col), f32),
+        p=vmem((Z, Y, group, d.col), bf16),
+        yin=vmem((Z, group, d.col), bf16),
+        zsrc=vmem((Z, group, d.col), bf16),
+        zin=vmem((Z, group, d.col), bf16),
+        hid=vmem((E, group, d.width), bf16),
+        ss=vmem((d.tokens, 128), f32),
+        racc=vmem((d.tokens, d.experts), f32),
+        gacc=vmem((d.tokens, hidden), f32),
+        uacc=vmem((d.tokens, hidden), f32),
+        acts=vmem((d.tokens, hidden), bf16),
+        pair=vmem((n, d.tokens // 2, d.out_width), bf16),
+        s1=vmem((n, 2, Y, d.tokens // 8, d.out_width), bf16),
+        h1=vmem((n, 2, d.tokens // 8, d.out_width), bf16),
+        s2=vmem((n, 2, d.tokens // 8, d.out_width), bf16),
+        h2=vmem((n, d.tokens // 8, d.out_width), bf16),
+        total=vmem((d.tokens // 8, d.out_width), f32),
+        zo=vmem((n, Z, d.tok, d.out_width), bf16),
+        zi=vmem((n, Z, d.tok, d.out_width), bf16),
+        load=dma((14,)),
+        k_send=dma((2, 3)), k_recv=dma((2, 3)),
+        r_send=dma((C,)), r_recv=dma((C,)),
+        n_send=dma((E,)), n_recv=dma((E,)),
+        m_send=dma((C,)), m_recv=dma((C,)),
+        h_send=dma((3, GROUPS)), h_recv=dma((3, GROUPS)),
+        y_send=dma((q,)), y_recv=dma((q,)),
+        z_send=dma((q, Z)), z_recv=dma((q, Z)),
+        g_send=dma((q, len(d.slot))), g_recv=dma((q, len(d.slot))),
+        p_send=dma((n,)), p_recv=dma((n,)),
+        a_send=dma((n,)), a_recv=dma((n,)),
+        b_send=dma((n,)), b_recv=dma((n,)),
+        e_send=dma((n, Z)), e_recv=dma((n, Z)),
+    )
+    anywhere = pl.BlockSpec(memory_space=pl.ANY)
+    operands = (
+        q_nope.reshape(queries, d.lat), q_rope, cache_keys, fresh_keys.T, block_order, w_uv, w_out,
+        residual, norm_gain.reshape(1, -1), router_weight.T, expert_ids, w_gate, w_up,
+        w_down.reshape(hidden, d.width),
+    )
+    return pl.pallas_call(
+        functools.partial(fused_kernel, tuple(scratch), d),
+        out_shape=jax.ShapeDtypeStruct(residual.shape, bf16),
+        in_specs=[anywhere] * len(operands),
+        out_specs=pl.BlockSpec(memory_space=pltpu.VMEM),
+        scratch_shapes=list(scratch.values()),
+        compiler_params=pltpu.CompilerParams(
+            collective_id=0, has_side_effects=True, vmem_limit_bytes=67043328
+        ),
+    )(*operands)
+
+
+def body(*arguments):
+    (
+        q_nope, q_rope, cache_keys, _, block_order, w_uv, w_out, residual, _, router_weight,
+        expert_ids, w_gate, _, _,
+    ) = arguments
+    ctx_count, exp_count = lax.axis_size("ctx"), lax.axis_size("exp")
+    rows, heads, lat = q_nope.shape
+    tokens = rows * ctx_count
+    block = tokens // block_order.shape[0]
+    if not fits(ctx_count, exp_count, q_nope, cache_keys, w_uv, w_out, residual, w_gate, block):
+        return staged_body(*arguments)
+    depth = exp_count // FOLD
+    steps = [("z", j) for j in range(1, depth)] + [("a", j) for j in range(depth)]
+    steps += [("b", j) for j in range(2 * depth)] + [("d", j) for j in range(4 * depth)]
+    width = residual.shape[1]
+    dims = types.SimpleNamespace(
+        ctx_count=ctx_count, exp_count=exp_count, rows=rows, heads=heads, lat=lat,
+        rope=q_rope.shape[1] // heads, vals=w_uv.shape[2], col=w_out.shape[1],
+        tok=residual.shape[0], tokens=tokens, cached=cache_keys.shape[1], top=expert_ids.shape[1],
+        block=block, experts=router_weight.shape[1], local=w_gate.shape[0], units=w_gate.shape[2],
+        width=width, chunks=widths(w_out.shape[1], 256, 2),
+        out_width=1024,
+        slot={step: i for i, step in enumerate(steps)},
+    )
+    return fused_body(dims, arguments)
+
+
 def solution(mesh):
     return jax.shard_map(
         body,

time: 118 us -> 76.4 us (0.65)
  matrix products: 27.9 us -> 0 us
  local copies, waits for them, and re-layouts: 8.98 us -> 1.46 us
  other arithmetic: 3.7 us -> 0 us
  Pallas kernels: 76.3 us -> 74.8 us
    dot_general x10 -> x0, matrix products: 27.9 us -> none  [the longest x2 8.73 us: body(): upward = jnp.dot(normed, w_up[i], preferred_element_type=jnp.float32)]
    reshape x8 -> x0, local copies, waits for them, and re-layouts: 3.36 us -> none  [the longest x1 1.65 us: attend(): query_pe.reshape(row_count * head_count, pe_width)]
    reduce_sum x4 -> x0, other arithmetic: 2.43 us -> none  [the longest x2 1.63 us: block_position(): leading = jnp.sum(jnp.where(lookup, block_order[None, :], 0), axis=1)]
    unnamed x29 -> x1, local copies, waits for them, and re-layouts: 3.87 us -> 1.46 us
    pallas_call x4 -> x1, Pallas kernels: 76.3 us -> 74.8 us  [fused_body(): pl.pallas_call(functools.partial(fused_kernel, tuple(scratch), d), out_sh...]
    div x2 -> x0, local copies, waits for them, and re-layouts: 1.48 us -> none  [body(): normal_lat = (latent / row_sum[:, :, None]).astype(jnp.bfloat16)]
where the time goes in v1:
time: 76.4 us; the launch traced here: 76.2 us
  Pallas kernels  74.8 us (98%)
  local copies, waits for them, and re-layouts  1.46 us (2%)
    pallas_call x1, Pallas kernels, fused_body(): pl.pallas_call(functools.partial(fused_kernel, tuple(scratch), d), out_sh...  74.8 us

profile of v1, /device:TPU:0, one launch (start us, length us, event | category | flops | bytes accessed | tf_op | source)
XLA Modules:
  0.0 76.2 jit_solution(7071964954387838722)
XLA Ops:
  0.0 74.8 %shard_map.136 = bf16[4,7168]{1,0:T(4,128)(2,1)} custom-call(bf16[512,512]{1,0:T(8,128)(2,1)} %bitcast.6, bf16[32,1024]{1,0:T(8,128)(2,1)} %q_rope.1, bf16[576,128]{1,0:T(8,128)(2,1)} %cache.1, bf16[32,576]{1,0:T(8,128)(2,1)} %bitcast.8, s32[8]{0:T(128)} %order.1, bf16[16,512,128]{2,1,0:T(8,128)(2,1)} %w_uv.1, bf16[2048,1792]{1,0:T(8,128)(2,1)} %w_out.1, ...), custom_call_target="tpu_custom_call" | custom-call | tf_op jit(solution)/shard_map/pallas_call | solution.py:993
  74.8 1.5 %copy.16 = bf16[4,7168]{1,0:T(4,128)(2,1)} copy(bf16[4,7168]{1,0:T(4,128)(2,1)} %shard_map.136) | data formatting | bytes 114688

commit v2 on v1

--- a/solution.py
+++ b/solution.py
@@ -495,8 +495,16 @@
     )
 
 
+def quo(i, n):
+    return lax.shift_right_logical(i, n.bit_length() - 1) if n & (n - 1) == 0 else i // n
+
+
+def rem(i, n):
+    return i & (n - 1) if n & (n - 1) == 0 else i % n
+
+
 def onehot(shape, source):
-    row = lax.broadcasted_iota(jnp.int32, shape, 0)
+    row = lax.broadcasted_iota(jnp.int32, (shape[0], 1), 0)
     col = lax.broadcasted_iota(jnp.int32, shape, 1)
     return jnp.where(col == source(row), 1.0, 0.0).astype(jnp.bfloat16)
 
@@ -507,6 +515,41 @@
 
 def mm_t(a, b):
     return lax.dot_general(a, b, (((1,), (1,)), ((), ())), preferred_element_type=jnp.float32)
+
+
+class Plan:
+    rates = dict(x=46e3, y=46e3, z=35e3, d=600e3)
+    delays = dict(x=2.0, y=2.0, z=2.6, d=1.1)
+
+    def __init__(self):
+        self.now, self.free, self.landed, self.tasks = 0.0, {}, {}, []
+
+    def note(self, key, link, size):
+        done = max(self.free.get(link, 0.0), self.now) + size / self.rates[link]
+        self.free[link] = done
+        self.landed[key] = done + self.delays[link]
+
+    def task(self, name, run, needs=(), after=(), cost=0.05, idle=False):
+        self.tasks.append((name, run, tuple(needs), tuple(after), cost, idle))
+
+    def run(self):
+        left, done, order = list(self.tasks), set(), []
+        while left:
+            best = None
+            for rank, (name, _, needs, after, cost, idle) in enumerate(left):
+                if all(a in done for a in after) and all(k in self.landed for k in needs):
+                    ready = max([self.landed[k] for k in needs] + [self.now])
+                    key = (ready, idle, rank)
+                    if best is None or key < best:
+                        best = key
+            ready, _, rank = best
+            name, run, _, _, cost, _ = left.pop(rank)
+            self.now = ready + cost
+            run()
+            done.add(name)
+            order.append((round(self.now, 2), name))
+        self.tasks = []
+        return order
 
 
 def fused_kernel(
@@ -532,8 +575,12 @@
     hg = heads // GROUPS
     sent = []
 
-    def push(src, dst, sems, index, target):
+    plan = Plan()
+
+    def push(src, dst, sems, index, target, key=None, link=None, size=0):
         send, recv = sems
+        if key is not None:
+            plan.note(key, link, 2.0 * size)
         copy = remote(src, dst, send.at[index], recv.at[index], target)
         copy.start()
         sent.append(copy)
@@ -557,10 +604,17 @@
     l_gain = load(gain, s.gain, 8)
     l_router = load(router, s.router, 9)
     l_out = load(w_out, s.wout, 10)
-    l_gate = load(w_gate, s.wg, 11)
-    l_up = load(w_up, s.wu, 12)
-    l_down = load(w_down, s.wd, 13)
-    greet(True)
+    barrier = pltpu.get_barrier_semaphore()
+    inner_left, inner_right = z > 0, z < Z - 1
+    left, right = (ctx, (z - 1) * FOLD + y), (ctx, (z + 1) * FOLD + y)
+    hail = functools.partial(pl.semaphore_signal, inc=1, device_id_type=pl.DeviceIdType.MESH)
+    count_of = lambda a, b: a.astype(jnp.int32) + b.astype(jnp.int32)
+    for k in range(1, C):
+        hail(barrier, device_id=((ctx + k) % C, exp))
+    hail(barrier, device_id=ypeer)
+    pl.when(inner_left)(lambda: hail(barrier, device_id=left))
+    pl.when(inner_right)(lambda: hail(barrier, device_id=right))
+    pl.semaphore_wait(barrier, C + count_of(inner_left, inner_right))
 
     l_cache.wait()
     l_fresh.wait()
@@ -589,16 +643,22 @@
         named = named + jnp.where(s.ids[:, k : k + 1] == lane, 1.0, 0.0)
     s.nsrc[...] = jnp.zeros((8, 128), f32)
     s.nsrc[0:tok, :] = named
+    s.nall[exp, ctx] = s.nsrc[...]
+    for r in range(2, Z):
+        tell_right = jnp.logical_and(z >= r - 1, inner_right)
+        tell_left = jnp.logical_and(z <= Z - r, inner_left)
+        pl.when(tell_right)(lambda r=r: hail(s.relay.at[0, r], device_id=right))
+        pl.when(tell_left)(lambda r=r: hail(s.relay.at[1, r], device_id=left))
+        pl.when(z >= r)(lambda r=r: pl.semaphore_wait(s.relay.at[0, r], 1))
+        pl.when(z <= Z - 1 - r)(lambda r=r: pl.semaphore_wait(s.relay.at[1, r], 1))
     n_flights = [
-        push(s.nsrc, s.nall.at[exp, ctx], (s.n_send, s.n_recv), k, (ctx, (exp + k) % E))
-        for k in range(1, E)
+        push(s.nsrc, s.nall.at[exp, ctx], (s.n_send, s.n_recv), k, zpeer(k)) for k in range(1, Z)
     ]
-    s.nall[exp, ctx] = s.nsrc[...]
 
     l_q.wait()
     for g in range(GROUPS):
         part = hg * rows
-        perm = onehot((part, rows * heads), lambda i: (i % rows) * heads + g * hg + i // rows)
+        perm = onehot((part, rows * heads), lambda i: rem(i, rows) * heads + g * hg + quo(i, rows))
         s.qh[g * part : (g + 1) * part, :] = mm(perm, s.qn[...]).astype(bf16)
     l_qr.wait()
     for h in range(heads):
@@ -608,22 +668,22 @@
     size = d.block
     own_blocks = rows // size
     part = hg * rows
-    row_id = lax.broadcasted_iota(jnp.int32, (part, tokens), 0) % rows
-    key_id = lax.broadcasted_iota(jnp.int32, (part, tokens), 1)
-    own_pos = row_id % size
-    key_pos = key_id % size
+    row_id = rem(lax.broadcasted_iota(jnp.int32, (part, 1), 0), rows)
+    key_id = lax.broadcasted_iota(jnp.int32, (1, tokens), 1)
+    own_pos = rem(row_id, size)
+    key_pos = rem(key_id, size)
     for b in range(own_blocks):
-        own_pos = own_pos + jnp.where(row_id // size == b, s.order[ctx * own_blocks + b] * size, 0)
+        own_pos = own_pos + jnp.where(quo(row_id, size) == b, s.order[ctx * own_blocks + b] * size, 0)
     for b in range(tokens // size):
-        key_pos = key_pos + jnp.where(key_id // size == b, s.order[b] * size, 0)
+        key_pos = key_pos + jnp.where(quo(key_id, size) == b, s.order[b] * size, 0)
     s.bias[...] = jnp.where(key_pos <= own_pos, 0.0, -jnp.inf)
-
-    for copy in n_flights:
-        copy.wait_recv()
-    n_last = []
-    for k in range(1, C):
-        view = s.nall.at[:, ctx]
-        n_last.append(push(view, view, (s.m_send, s.m_recv), k, ((ctx + k) % C, exp)))
+    l_uv.wait()
+    l_gain.wait()
+    l_router.wait()
+    l_out.wait()
+    l_gate = load(w_gate, s.wg, 11)
+    l_up = load(w_up, s.wu, 12)
+    l_down = load(w_down, s.wd, 13)
 
     for copy in k_cross:
         copy.wait_recv()
@@ -632,7 +692,6 @@
         copy.wait_recv()
 
     scale = 1.0 / math.sqrt(QKD)
-    l_uv.wait()
     h_cross, h_pair = [], []
     for g in range(GROUPS):
         q = s.qh[g * part : (g + 1) * part, :]
@@ -652,172 +711,202 @@
         view = s.heads.at[ctx, g]
         h_cross.append(push(view, view, (s.h_send, s.h_recv), (0, g), xpeer))
         h_pair.append(push(view, view, (s.h_send, s.h_recv), (1, g), partner))
+    for copy in n_flights:
+        copy.wait_recv()
+    named_y = []
+    for j in range(Z):
+        view = s.nall.at[(z + Z - j) % Z * FOLD + y, ctx]
+        named_y.append(push(view, view, (s.o_send, s.o_recv), j, ypeer))
     h_far = []
     for g in range(GROUPS):
         h_cross[g].wait_recv()
         view = s.heads.at[xctx, g]
         h_far.append(push(view, view, (s.h_send, s.h_recv), (2, g), partner))
 
-    l_out.wait()
     deep = hg * vals
-    for g in range(GROUPS):
+    for g in range(GROUPS - 1):
         h_pair[g].wait_recv()
         h_far[g].wait_recv()
         value = mm(s.heads[:, g].reshape(tokens, deep), s.wout[g * deep : (g + 1) * deep, :])
-        if g == 0:
-            s.pacc[...] = value
-        else:
-            s.pacc[...] = s.pacc[...] + value
+        s.pacc[...] = value if g == 0 else s.pacc[...] + value
+    h_pair[GROUPS - 1].wait_recv()
+    h_far[GROUPS - 1].wait_recv()
+
+    for copy in named_y:
+        copy.wait_recv()
+    n_last = []
+    for k in range(1, C):
+        view = s.nall.at[:, ctx]
+        n_last.append(push(view, view, (s.m_send, s.m_recv), k, ((ctx + k) % C, exp)))
 
     chunks = d.chunks
     starts = offsets(chunks)
     to_group = onehot(
-        (tokens, tokens), lambda i: (i // tok) % C * rows + i // group * tok + i % tok
-    )
-    y_flights = []
-    for q, (o, w) in enumerate(zip(starts, chunks)):
-        value = mm(to_group, s.pacc[:, o : o + w].astype(bf16)).astype(bf16)
+        (tokens, tokens), lambda i: rem(quo(i, tok), C) * rows + quo(i, group) * tok + rem(i, tok)
+    )
+    flights = {}
+    count = len(chunks)
+    ahead = d.ahead
+
+    def open_sum(q):
+        o, w = starts[q], chunks[q]
+        value = s.pacc[:, o : o + w] + mm(
+            s.heads[:, GROUPS - 1].reshape(tokens, deep), s.wout[(GROUPS - 1) * deep :, o : o + w]
+        )
+        value = mm(to_group, value.astype(bf16)).astype(bf16)
         s.p[:, :, :, o : o + w] = value.reshape(Z, FOLD, group, w)
-        y_flights.append(
-            push(
-                s.p.at[:, 1 - y, :, pl.ds(o, w)], s.yin.at[:, :, pl.ds(o, w)],
-                (s.y_send, s.y_recv), q, ypeer,
-            )
+        flights["y", q] = push(
+            s.p.at[:, 1 - y, :, pl.ds(o, w)], s.yin.at[:, :, pl.ds(o, w)],
+            (s.y_send, s.y_recv), q, ypeer, ("y", q), "y", Z * group * w,
         )
-    z_flights = []
-    for q, (o, w) in enumerate(zip(starts, chunks)):
-        y_flights[q].wait_recv()
+
+    def sum_y(q):
+        o, w = starts[q], chunks[q]
+        flights["y", q].wait_recv()
         both = s.p[:, y, :, o : o + w].astype(f32) + s.yin[:, :, o : o + w].astype(f32)
         s.zsrc[:, :, o : o + w] = both.astype(bf16)
-        z_flights.append([
-            push(
+        for j in range(1, Z):
+            flights["z", q, j] = push(
                 s.zsrc.at[(z + j) % Z, :, pl.ds(o, w)], s.zin.at[j, :, pl.ds(o, w)],
-                (s.z_send, s.z_recv), (q, j), zpeer(j),
+                (s.z_send, s.z_recv), (q, j), zpeer(j), ("z", q, j), "z", group * w,
             )
-            for j in range(1, Z)
-        ])
-    for copy in r_flights:
-        copy.wait_recv()
-    for c in range(C):
-        s.rsum[c * tok : (c + 1) * tok, :] = s.rin[c].astype(f32)
+
+    def add_residual():
+        for copy in r_flights:
+            copy.wait_recv()
+        for c in range(C):
+            s.rsum[c * tok : (c + 1) * tok, :] = s.rin[c].astype(f32)
 
     def block(c, e, q):
         return s.hid.at[e, :, lanes(c * col + starts[q], chunks[q])]
 
-    gather = {}
-
     def spread(q, step, index, c, e, target):
         view = block(c, e, q)
-        gather[q, step, index] = push(view, view, (s.g_send, s.g_recv), (q, d.slot[step, index]), target)
+        link = step if step in "zd" else ("y" if (step == "a") == ahead[q] else "x")
+        flights["g" + step, q, index] = push(
+            view, view, (s.g_send, s.g_recv), (q, d.slot[step, index]), target,
+            ("g" + step, q, index), link, group * chunks[q],
+        )
 
     def axes(q):
-        return (ypeer, xpeer) if q % 2 == 0 else (xpeer, ypeer)
+        return (ypeer, xpeer) if ahead[q] else (xpeer, ypeer)
 
     def near(q, j):
         return ctx, (z + Z - j) % Z * FOLD + y
 
     def first(q, j):
         c, e = near(q, j)
-        return (c, e + 1 - 2 * y) if q % 2 == 0 else (xctx, e)
+        return (c, e + 1 - 2 * y) if ahead[q] else (xctx, e)
 
     def second(q, i):
-        if q % 2 == 0:
-            return xctx, (near(q, i) if i < Z else first(q, i - Z))[1]
         c, e = near(q, i) if i < Z else first(q, i - Z)
-        return c, e + 1 - 2 * y
-
-    def open_gather(q):
+        return (xctx, e) if ahead[q] else (c, e + 1 - 2 * y)
+
+    def sum_z(q):
+        o, w = starts[q], chunks[q]
+        both = s.p[z, y, :, o : o + w].astype(f32) + s.yin[z, :, o : o + w].astype(f32)
+        for j in range(1, Z):
+            flights["z", q, j].wait_recv()
+            both = both + s.zin[j, :, o : o + w].astype(f32)
+        both = both + s.rsum[:, o : o + w]
+        s.hid[exp, :, lanes(ctx * col + o, w)] = both.astype(bf16)
         c, e = near(q, 0)
+        a, b = axes(q)
         for j in range(1, Z):
             spread(q, "z", j, c, e, zpeer(j))
-        a, b = axes(q)
         spread(q, "a", 0, c, e, a)
         spread(q, "b", 0, c, e, b)
         spread(q, "d", 0, c, e, partner)
 
-    def pass_near(q):
+    def pass_near(q, j):
         a, b = axes(q)
+        flights["gz", q, j].wait_recv()
+        c, e = near(q, j)
+        spread(q, "a", j, c, e, a)
+        spread(q, "b", j, c, e, b)
+        spread(q, "d", j, c, e, partner)
+
+    def pass_first(q, j):
+        _, b = axes(q)
+        flights["ga", q, j].wait_recv()
+        c, e = first(q, j)
+        spread(q, "b", Z + j, c, e, b)
+        spread(q, "d", Z + j, c, e, partner)
+
+    def pass_second(q, i):
+        flights["gb", q, i].wait_recv()
+        c, e = second(q, i)
+        spread(q, "d", 2 * Z + i, c, e, partner)
+
+    units = d.units
+
+    def open_units():
+        l_gate.wait()
+        l_up.wait()
+        s.ss[...] = jnp.zeros(s.ss.shape, f32)
+        s.racc[...] = jnp.zeros(s.racc.shape, f32)
+        s.gacc[...] = jnp.zeros(s.gacc.shape, f32)
+        s.uacc[...] = jnp.zeros(s.uacc.shape, f32)
+
+    def consume(q, c, arrivals):
+        for key in arrivals:
+            flights[key].wait_recv()
+        w = chunks[q]
+        at = lanes(c * col + starts[q], w)
+        hidden = s.hid[:, :, at].reshape(tokens, w).astype(f32)
+        square = hidden * hidden
+        some = square[:, 0:128]
+        for k in range(1, w // 128):
+            some = some + square[:, k * 128 : (k + 1) * 128]
+        s.ss[...] = s.ss[...] + some
+        scaled = (hidden * s.gain[:, at]).astype(bf16)
+        s.racc[...] = s.racc[...] + mm_t(scaled, s.router[:, at])
+        for k in range(d.local):
+            here = slice(k * units, (k + 1) * units)
+            s.gacc[:, here] = s.gacc[:, here] + mm(scaled, s.wg[k, at, :])
+            s.uacc[:, here] = s.uacc[:, here] + mm(scaled, s.wu[k, at, :])
+
+    call = functools.partial
+    plan.task("residual", add_residual, cost=0.3)
+    for q in range(count):
+        w = chunks[q] / 512
+        plan.task(("o", q), call(open_sum, q), after=[("o", q - 1)] if q else [], cost=0.15 * w)
+    plan.task("units", open_units, cost=0.3, idle=True)
+    for q in range(count):
+        w = chunks[q] / 512
+        plan.task(("sy", q), call(sum_y, q), [("y", q)], cost=0.2 * w)
+        plan.task(
+            ("sz", q), call(sum_z, q), [("z", q, j) for j in range(1, Z)],
+            ["residual", ("sy", q)], cost=0.15 * w,
+        )
         for j in range(1, Z):
-            gather[q, "z", j].wait_recv()
-            c, e = near(q, j)
-            spread(q, "a", j, c, e, a)
-            spread(q, "b", j, c, e, b)
-            spread(q, "d", j, c, e, partner)
-
-    def pass_first(q):
-        _, b = axes(q)
+            plan.task(("n", q, j), call(pass_near, q, j), [("gz", q, j)], [("sz", q)])
         for j in range(Z):
-            gather[q, "a", j].wait_recv()
-            c, e = first(q, j)
-            spread(q, "b", Z + j, c, e, b)
-            spread(q, "d", Z + j, c, e, partner)
-
-    def pass_second(q):
+            plan.task(("f", q, j), call(pass_first, q, j), [("ga", q, j)], [("sz", q)])
         for i in range(2 * Z):
-            gather[q, "b", i].wait_recv()
-            c, e = second(q, i)
-            spread(q, "d", 2 * Z + i, c, e, partner)
-
-    def close_gather(q):
-        for i in range(4 * Z):
-            gather[q, "d", i].wait_recv()
-
-    for q, (o, w) in enumerate(zip(starts, chunks)):
-        for copy in z_flights[q]:
-            copy.wait_recv()
-        both = s.p[z, y, :, o : o + w].astype(f32) + s.yin[z, :, o : o + w].astype(f32)
-        for j in range(1, Z):
-            both = both + s.zin[j, :, o : o + w].astype(f32)
-        both = both + s.rsum[:, o : o + w]
-        s.hid[exp, :, lanes(ctx * col + o, w)] = both.astype(bf16)
-        open_gather(q)
-
-    l_gain.wait()
-    l_router.wait()
-    l_gate.wait()
-    l_up.wait()
-    s.ss[...] = jnp.zeros(s.ss.shape, f32)
-    s.racc[...] = jnp.zeros(s.racc.shape, f32)
-    s.gacc[...] = jnp.zeros(s.gacc.shape, f32)
-    s.uacc[...] = jnp.zeros(s.uacc.shape, f32)
-    units = d.units
-
-    def consume(q):
-        w = chunks[q]
-
-        def one(i, carry):
-            c = (ctx + i) % C
-            at = lanes(c * col + starts[q], w)
-            hidden = s.hid[:, :, at].reshape(tokens, w).astype(f32)
-            square = hidden * hidden
-            some = square[:, 0:128]
-            for k in range(1, w // 128):
-                some = some + square[:, k * 128 : (k + 1) * 128]
-            s.ss[...] = s.ss[...] + some
-            scaled = (hidden * s.gain[:, at]).astype(bf16)
-            s.racc[...] = s.racc[...] + mm_t(scaled, s.router[:, at])
-            for k in range(d.local):
-                here = slice(k * units, (k + 1) * units)
-                s.gacc[:, here] = s.gacc[:, here] + mm(scaled, s.wg[k, at, :])
-                s.uacc[:, here] = s.uacc[:, here] + mm(scaled, s.wu[k, at, :])
-            return carry
-
-        lax.fori_loop(0, C, one, 0)
-
-    count = len(chunks)
-    for q in range(count):
-        pass_near(q)
-        pass_first(q)
-    for q in range(count):
-        pass_second(q)
-        close_gather(q)
-        if q > 0:
-            consume(q - 1)
-    consume(count - 1)
+            plan.task(("s", q, i), call(pass_second, q, i), [("gb", q, i)], [("sz", q)])
+        nears = [("sz", q)] + [("n", q, j) for j in range(1, Z)]
+        firsts = [("f", q, j) for j in range(Z)]
+        seconds = [("s", q, i) for i in range(2 * Z)]
+        if ahead[q]:
+            mine, theirs = nears + firsts, seconds
+            own_d = list(range(2 * Z))
+        else:
+            mine, theirs = nears + seconds[:Z], firsts + seconds[Z:]
+            own_d = list(range(Z)) + list(range(2 * Z, 3 * Z))
+        far_d = [i for i in range(4 * Z) if i not in own_d]
+        pair_c, far_c = ctx + 1 - 2 * core, xctx + 1 - 2 * core
+        near_keys, far_keys = [("gd", q, i) for i in own_d], [("gd", q, i) for i in far_d]
+        late = dict(cost=0.4 * w, idle=True)
+        plan.task(("c", q, 0), call(consume, q, ctx, []), [], mine + ["units"], **late)
+        plan.task(("c", q, 1), call(consume, q, pair_c, near_keys), near_keys, ["units"], **late)
+        plan.task(("c", q, 2), call(consume, q, xctx, []), [], theirs + ["units"], **late)
+        plan.task(("c", q, 3), call(consume, q, far_c, far_keys), far_keys, ["units"], **late)
+    trail = plan.run()
 
     for copy in n_last:
         copy.wait_recv()
-    squeeze = onehot((tokens, tokens // tok * 8), lambda i: i // tok * 8 + i % tok)
+    squeeze = onehot((tokens, tokens // tok * 8), lambda i: quo(i, tok) * 8 + rem(i, tok))
     named = mm(squeeze, s.nall[...].reshape(tokens // tok * 8, 128).astype(bf16))
     named = named[:, 0 : d.experts]
     mean = jnp.sum(s.ss[...], axis=1, keepdims=True) * (1.0 / d.width)
@@ -834,8 +923,8 @@
         s.acts[:, here] = (gate * jax.nn.sigmoid(gate) * upward * mine).astype(bf16)
 
     def owner_order(i):
-        t, zz, yy = i % tok, i // tok % Z, i // (tok * Z) % FOLD
-        xx, kk = i // (tok * Z * FOLD) % 2, i // (tok * Z * FOLD * 2)
+        t, zz, yy = rem(i, tok), rem(quo(i, tok), Z), rem(quo(i, tok * Z), FOLD)
+        xx, kk = rem(quo(i, tok * Z * FOLD), 2), quo(i, tok * Z * FOLD * 2)
         return (zz * FOLD + yy) * group + (xx * 2 + kk) * tok + t
 
     to_owner = onehot((tokens, tokens), owner_order)
@@ -851,7 +940,7 @@
         mixed = mm(s.acts[...], s.wd[:, i * cw : (i + 1) * cw]).astype(bf16)
         s.wout[i * tokens : (i + 1) * tokens, 0:cw] = mixed
         away = s.wout.at[pl.ds(pl.multiple_of(i * tokens + (1 - core) * half, 16), half), pl.ds(0, cw)]
-        pairs[i] = push(away, s.pair.at[i], (s.p_send, s.p_recv), i, partner)
+        pairs[i] = push(away, s.pair.at[i], (s.p_send, s.p_recv), i, partner, ("p", i), "d", half * cw)
 
     def join_pair(i):
         pairs[i].wait_recv()
@@ -859,18 +948,30 @@
         both = mine.astype(f32) + s.pair[i].astype(f32)
         s.s1[i] = both.astype(bf16).reshape(2, FOLD, eighth, cw)
         if i % 2 == 0:
-            hops[i] = push(s.s1.at[i, 1 - x], s.h1.at[i], (s.a_send, s.a_recv), i, xpeer)
+            hops[i] = push(
+                s.s1.at[i, 1 - x], s.h1.at[i], (s.a_send, s.a_recv), i, xpeer,
+                ("a", i), "x", quarter * cw,
+            )
         else:
-            hops[i] = push(s.s1.at[i, :, 1 - y], s.h1.at[i], (s.a_send, s.a_recv), i, ypeer)
+            hops[i] = push(
+                s.s1.at[i, :, 1 - y], s.h1.at[i], (s.a_send, s.a_recv), i, ypeer,
+                ("a", i), "y", quarter * cw,
+            )
 
     def join_hop(i):
         hops[i].wait_recv()
         mine = s.s1[i, x] if i % 2 == 0 else s.s1[i, :, y]
         s.s2[i] = (mine.astype(f32) + s.h1[i].astype(f32)).astype(bf16)
         if i % 2 == 0:
-            lasts[i] = push(s.s2.at[i, 1 - y], s.h2.at[i], (s.b_send, s.b_recv), i, ypeer)
+            lasts[i] = push(
+                s.s2.at[i, 1 - y], s.h2.at[i], (s.b_send, s.b_recv), i, ypeer,
+                ("b", i), "y", eighth * cw,
+            )
         else:
-            lasts[i] = push(s.s2.at[i, 1 - x], s.h2.at[i], (s.b_send, s.b_recv), i, xpeer)
+            lasts[i] = push(
+                s.s2.at[i, 1 - x], s.h2.at[i], (s.b_send, s.b_recv), i, xpeer,
+                ("b", i), "x", eighth * cw,
+            )
 
     def join_last(i):
         lasts[i].wait_recv()
@@ -879,7 +980,10 @@
         for zz in range(Z):
             s.zo[i, zz] = s.total[zz * tok : (zz + 1) * tok, :].astype(bf16)
         ends[i] = [
-            push(s.zo.at[i, (z + j) % Z], s.zi.at[i, j], (s.e_send, s.e_recv), (i, j), zpeer(j))
+            push(
+                s.zo.at[i, (z + j) % Z], s.zi.at[i, j], (s.e_send, s.e_recv), (i, j), zpeer(j),
+                ("e", i, j), "z", tok * cw,
+            )
             for j in range(1, Z)
         ]
 
@@ -894,19 +998,14 @@
             value = value + s.zi[i, j].astype(f32)
         out[:, at] = value.astype(bf16)
 
-    lag = 3
     for i in range(n):
-        produce(i)
-        if i >= lag:
-            join_pair(i - lag)
-    for i in range(max(n - lag, 0), n):
-        join_pair(i)
-    for i in range(n):
-        join_hop(i)
-    for i in range(n):
-        join_last(i)
-    for i in range(n):
-        finish(i)
+        plan.task(("o", i), call(produce, i), after=[("o", i - 1)] if i else [], cost=0.35, idle=True)
+        plan.task(("p", i), call(join_pair, i), [("p", i)], cost=0.25)
+        plan.task(("a", i), call(join_hop, i), [("a", i)], cost=0.15)
+        plan.task(("b", i), call(join_last, i), [("b", i)], cost=0.1)
+        plan.task(("e", i), call(finish, i), [("e", i, j) for j in range(1, Z)], cost=0.05)
+    trail = trail + plan.run()
+
     for copy in sent:
         copy.wait_send()
 
@@ -973,7 +1072,9 @@
         load=dma((14,)),
         k_send=dma((2, 3)), k_recv=dma((2, 3)),
         r_send=dma((C,)), r_recv=dma((C,)),
-        n_send=dma((E,)), n_recv=dma((E,)),
+        n_send=dma((Z,)), n_recv=dma((Z,)),
+        o_send=dma((Z,)), o_recv=dma((Z,)),
+        relay=pltpu.SemaphoreType.REGULAR((2, Z)),
         m_send=dma((C,)), m_recv=dma((C,)),
         h_send=dma((3, GROUPS)), h_recv=dma((3, GROUPS)),
         y_send=dma((q,)), y_recv=dma((q,)),
@@ -984,6 +1085,12 @@
         b_send=dma((n,)), b_recv=dma((n,)),
         e_send=dma((n, Z)), e_recv=dma((n, Z)),
     )
+    held = SPARE_BYTES // 2 + sum(
+        math.prod(k.shape[:-2]) * -(-k.shape[-2] // 8) * 8 * -(-k.shape[-1] // 128) * 128
+        * jnp.dtype(k.dtype).itemsize
+        for name, k in scratch.items()
+        if name != "order" and not name.endswith(("load", "_send", "_recv", "relay"))
+    )
     anywhere = pl.BlockSpec(memory_space=pl.ANY)
     operands = (
         q_nope.reshape(queries, d.lat), q_rope, cache_keys, fresh_keys.T, block_order, w_uv, w_out,
@@ -997,7 +1104,7 @@
         out_specs=pl.BlockSpec(memory_space=pltpu.VMEM),
         scratch_shapes=list(scratch.values()),
         compiler_params=pltpu.CompilerParams(
-            collective_id=0, has_side_effects=True, vmem_limit_bytes=67043328
+            collective_id=0, has_side_effects=True, vmem_limit_bytes=min(held, 67043328)
         ),
     )(*operands)
 
@@ -1022,7 +1129,7 @@
         rope=q_rope.shape[1] // heads, vals=w_uv.shape[2], col=w_out.shape[1],
         tok=residual.shape[0], tokens=tokens, cached=cache_keys.shape[1], top=expert_ids.shape[1],
         block=block, experts=router_weight.shape[1], local=w_gate.shape[0], units=w_gate.shape[2],
-        width=width, chunks=widths(w_out.shape[1], 256, 2),
+        width=width, chunks=widths(w_out.shape[1], 256, 4), ahead=[True, False] * 2,
         out_width=1024,
         slot={step: i for i, step in enumerate(steps)},
     )

time: 76.4 us -> 67.7 us (0.89)
  Pallas kernels: 74.8 us -> 66.1 us
    pallas_call x1, Pallas kernels: 74.8 us -> 66.1 us  [fused_body(): pl.pallas_call(functools.partial(fused_kernel, tuple(scratch), d), out_sh...]
where the time goes in v2:
time: 67.7 us; the launch traced here: 67.6 us
  Pallas kernels  66.1 us (98%)
  local copies, waits for them, and re-layouts  1.46 us (2%)
    pallas_call x1, Pallas kernels, fused_body(): pl.pallas_call(functools.partial(fused_kernel, tuple(scratch), d), out_sh...  66.1 us
    unnamed x1, local copies, waits for them, and re-layouts  1.46 us

profile of v2, /device:TPU:0, one launch (start us, length us, event | category | flops | bytes accessed | tf_op | source)
XLA Modules:
  0.0 67.6 jit_solution(433756840878655663)
XLA Ops:
  0.0 66.1 %shard_map.136 = bf16[4,7168]{1,0:T(4,128)(2,1)} custom-call(bf16[512,512]{1,0:T(8,128)(2,1)} %bitcast.6, bf16[32,1024]{1,0:T(8,128)(2,1)} %q_rope.1, bf16[576,128]{1,0:T(8,128)(2,1)} %cache.1, bf16[32,576]{1,0:T(8,128)(2,1)} %bitcast.8, s32[8]{0:T(128)} %order.1, bf16[16,512,128]{2,1,0:T(8,128)(2,1)} %w_uv.1, bf16[2048,1792]{1,0:T(8,128)(2,1)} %w_out.1, ...), custom_call_target="tpu_custom_call" | custom-call | tf_op jit(solution)/shard_map/pallas_call | solution.py:1100
  66.1 1.5 %copy.16 = bf16[4,7168]{1,0:T(4,128)(2,1)} copy(bf16[4,7168]{1,0:T(4,128)(2,1)} %shard_map.136) | data formatting | bytes 114688
